TPU v7x, 256 devices: a whole 4x4x8 slice. The times are simulated.
256 devices in a mesh: dp: 8 (over x, y_lo), tp: 32 (over y_hi, z, core).
Axes of the slice: x: 4, y: 4 (y_hi: 2, y_lo: 2; y = y_hi * 2 + y_lo), z: 8, core: 2. Of those that a mesh axis runs over, the one named last changes fastest.
Arguments:
- proj_in: bfloat16 [1, 32768, 8192], P(None, 'dp', 'tp'), may hold values from -6 to 6
- kv_grad: bfloat16 [1, 32768, 2048], P(None, ('dp', 'tp')), may hold values from -0.75 to 0.75
- normed: bfloat16 [1, 32768, 8192], P(None, ('dp', 'tp')), may hold values from -6 to 6
- norm_grad: bfloat16 [1, 32768, 8192], P(None, ('dp', 'tp')), may hold values from -0.6 to 0.6
- first_moment: float32 [1, 8192, 2048], P(None, 'tp', 'dp'), may hold values from -0.6 to 0.6
- second_moment: float32 [1, 8192, 2048], P(None, 'tp', 'dp'), may hold values from 0.002 to 0.02
Outputs:
- new_first: float32 [1, 8192, 2048], P(None, 'tp', 'dp')
- new_second: float32 [1, 8192, 2048], P(None, 'tp', 'dp')
- adam_step: float32 [1, 8192, 2048], P(None, 'tp', 'dp')
- gain_grad: float32 [1, 8192], replicated
All inputs are finite; a program needn't handle non-finite values.
Results may differ from a plain program's by a relative error of at most 0.0003.
Values may be sent and summed in bfloat16 or wider, within the bound.
A program may use at most 128 MiB of HBM per device.

v0:
```python
import functools
import jax
import jax.numpy as jnp
from jax import lax
from jax.sharding import Mesh
from jax.sharding import PartitionSpec as P

DP = ("dp_0", "dp_1")
DP_TP = ("dp_0", "dp_1", "tp_0", "tp_1", "tp_2")
TP = ("tp_0", "tp_1", "tp_2")
beta_one = 0.9
beta_two = 0.95
correct_one = 0.19
correct_two = 0.0975
epsilon = 1e-08


def over_axes(array, axes):
    return functools.reduce(lax.psum, axes, array)


def in_blocks(array, dim, size):
    lengths = array.shape
    pieces = array.reshape(*lengths[:dim], size, lengths[dim] // size, *lengths[dim + 1 :])
    return jnp.moveaxis(pieces, dim, 0)


def sent_and_summed(array, axis, dim):
    pieces = in_blocks(array, dim, lax.axis_size(axis))
    arrived = lax.all_to_all(pieces, axis, split_axis=0, concat_axis=0, tiled=True)
    return arrived.sum(axis=0)


def adam_update(mean_grad, first_old, second_old):
    new_first = beta_one * first_old + (1.0 - beta_one) * mean_grad
    new_second = beta_two * second_old + (1.0 - beta_two) * mean_grad * mean_grad
    update = new_first / correct_one / (jnp.sqrt(new_second / correct_two) + epsilon)
    return (new_first, new_second, update)


def row_adder(inputs, arrived):
    return lax.dot_general(
        inputs, arrived, (((0,), (0,)), ((), ())), preferred_element_type=jnp.float32
    )


def shards(proj_in, kv_grad, normed, norm_grad, first_moment, second_moment):
    replicas = lax.axis_size(DP)
    local_terms = jnp.sum(norm_grad.astype(jnp.float32) * normed.astype(jnp.float32), axis=1)
    gain_grad = over_axes(local_terms, DP_TP) / replicas
    inputs = proj_in[0]
    grad_rows = kv_grad[0]
    local_grad = row_adder(inputs, lax.all_gather(grad_rows, TP, axis=0, tiled=True))
    mean_grad = sent_and_summed(local_grad, DP, 1) / replicas
    new_first, new_second, update = adam_update(mean_grad, first_moment[0], second_moment[0])
    firsts = [new_first]
    seconds = [new_second]
    updates = [update]
    return (jnp.stack(firsts), jnp.stack(seconds), jnp.stack(updates), gain_grad)


def solution(mesh):
    finer = Mesh(mesh.devices.reshape(4, 2, 2, 8, 2), ("dp_0", "dp_1", "tp_0", "tp_1", "tp_2"))
    return jax.shard_map(
        shards,
        mesh=finer,
        in_specs=(
            P(None, DP, TP),
            P(None, DP_TP, None),
            P(None, DP_TP, None),
            P(None, DP_TP, None),
            P(None, TP, DP),
            P(None, TP, DP),
        ),
        out_specs=(P(None, TP, DP), P(None, TP, DP), P(None, TP, DP), P()),
        check_vma=False,
    )
```

profile of v0, /device:TPU:1, one launch (start us, length us, event | category | flops | bytes accessed | tf_op | source)
XLA Modules:
  0.0 229.3 jit_solution(13198261550055182338)
XLA Ops:
  7.2 0.0 copy-start
  7.2 0.0 all-gather.3.cloned.1.call-start
  7.2 0.7 all-gather.3.cloned.1.call-update
  7.9 2.8 %multiply_reduce_fusion = f32[8192]{0:T(1024)S(1)} fusion(bf16[1,128,8192]{2,1,0:T(8,128)(2,1)} %param.8, bf16[1,128,8192]{2,1,0:T(8,128)(2,1)} %param.9), kind=kLoop, calls=%fused_computation | loop fusion | flops 4186112 | bytes 4227072 | tf_op jit(solution)/shard_map/reduce_sum | solution.py:49
  10.7 14.3 %psum.35 = f32[1,8192]{1,0:T(1,128)S(1)} all-reduce(f32[1,8192]{1,0:T(1,128)S(1)} %bitcast.23), channel_id=1, replica_groups=mesh['dp_0'=4,'dp_1'=2,'tp_0'=2,'tp_1'=8,'tp_2'=2] {'dp_0'}, use_global_device_ids=true, to_apply=%region_2.0 | all-reduce | flops 8192 | bytes 65536 | tf_op jit(solution)/shard_map/psum | solution.py:19
  25.1 7.0 %psum.36 = f32[1,8192]{1,0:T(1,128)S(1)} all-reduce(f32[1,8192]{1,0:T(1,128)S(1)} %psum.35), channel_id=1, replica_groups=mesh['dp_0'=4,'dp_1'=2,'tp_0'=2,'tp_1'=8,'tp_2'=2] {'dp_1'}, use_global_device_ids=true, to_apply=%region_3.0 | all-reduce | flops 8192 | bytes 65536 | tf_op jit(solution)/shard_map/psum | solution.py:19
  32.1 9.2 %psum.37 = f32[1,8192]{1,0:T(1,128)S(1)} all-reduce(f32[1,8192]{1,0:T(1,128)S(1)} %psum.36), channel_id=1, replica_groups=mesh['dp_0'=4,'dp_1'=2,'tp_0'=2,'tp_1'=8,'tp_2'=2] {'tp_0'}, use_global_device_ids=true, to_apply=%region_4.0 | all-reduce | flops 8192 | bytes 65536 | tf_op jit(solution)/shard_map/psum | solution.py:19
  41.3 111.2 %all-gather.3.cloned.1.call-done = bf16[1,4096,2048]{2,1,0:T(8,128)(2,1)} async-done(((bf16[1,128,2048]{2,1,0:T(8,128)(2,1)}), bf16[1,4096,2048]{2,1,0:T(8,128)(2,1)}) %all-gather.3.cloned.1.call-update) | async-done | bytes 16777232 | tf_op jit(solution)/shard_map/all_gather | solution.py:53
  152.5 20.7 %copy.10 = bf16[2048,4096]{1,0:T(8,128)(2,1)} copy(bf16[2048,4096]{0,1:T(8,128)(2,1)} %bitcast.21) | data formatting | bytes 33554432 | tf_op jit(solution)/shard_map/dot_general | solution.py:42
  173.3 0.0 copy-done
  173.3 9.5 %fusion.2 = f32[8,256,256]{2,1,0:T(8,128)} fusion(bf16[8,256,4096]{2,1,0:T(8,128)(2,1)} %bitcast.22, bf16[1,4096,256]{2,1,0:T(8,128)(2,1)S(1)} %copy-done), kind=kOutput, calls=%fused_computation.3 | convolution fusion | flops 4294967296 | bytes 20971520 | tf_op jit(solution)/shard_map/dot_general | solution.py:42
  182.8 4.3 %all-to-all-start = ((f32[8,256,256]{2,1,0:T(8,128)}), f32[8,256,256]{2,1,0:T(8,128)}, u32[]{:S(2)}, u32[]{:S(2)}) async-start(f32[8,256,256]{2,1,0:T(8,128)} %fusion.2), calls=%async_computation | async-start | bytes 4194304 | tf_op jit(solution)/shard_map/all_to_all | solution.py:30
  187.1 0.0 copy-start.1
  187.2 0.0 copy-start.2
  187.2 24.0 %psum.38 = f32[1,8192]{1,0:T(1,128)S(1)} all-reduce(f32[1,8192]{1,0:T(1,128)S(1)} %psum.37), channel_id=1, replica_groups=mesh['dp_0'=4,'dp_1'=2,'tp_0'=2,'tp_1'=8,'tp_2'=2] {'tp_1'}, use_global_device_ids=true, to_apply=%region_5.0 | all-reduce | flops 8192 | bytes 65536 | tf_op jit(solution)/shard_map/psum | solution.py:19
  211.1 7.9 %psum.39 = f32[1,8192]{1,0:T(1,128)S(1)} all-reduce(f32[1,8192]{1,0:T(1,128)S(1)} %psum.38), channel_id=1, replica_groups=mesh['dp_0'=4,'dp_1'=2,'tp_0'=2,'tp_1'=8,'tp_2'=2] {'tp_2'}, use_global_device_ids=true, to_apply=%region_6.0 | all-reduce | flops 8192 | bytes 65536 | tf_op jit(solution)/shard_map/psum | solution.py:19
  219.1 0.6 broadcast_multiply_fusion
  219.7 0.0 all-to-all-done
  219.7 1.8 reduce_sum.20
  221.5 0.0 copy-done.1
  221.5 0.0 copy-done.2
  221.5 1.0 add_divide_fusion
Async XLA Ops:
  7.2 166.1 %copy-start = (bf16[1,4096,256]{2,1,0:T(8,128)(2,1)S(1)}, bf16[1,4096,256]{2,1,0:T(8,128)(2,1)}, u32[]{:S(2)}) copy-start(bf16[1,4096,256]{2,1,0:T(8,128)(2,1)} %param.6) | copy-start | bytes 6291460
  7.2 145.3 %all-gather.3.cloned.1.call-start = ((), (), s32[]{:S(2)}) async-start(), calls=%async_computation.1 | async-start | bytes 17301504 | tf_op jit(solution)/shard_map/all_gather | solution.py:53
  182.8 36.9 %all-to-all-start = ((f32[8,256,256]{2,1,0:T(8,128)}), f32[8,256,256]{2,1,0:T(8,128)}, u32[]{:S(2)}, u32[]{:S(2)}) async-start(f32[8,256,256]{2,1,0:T(8,128)} %fusion.2), calls=%async_computation | async-start | bytes 4194304 | tf_op jit(solution)/shard_map/all_to_all | solution.py:30
  187.1 34.3 %copy-start.1 = (f32[1,256,256]{2,1,0:T(8,128)S(1)}, f32[1,256,256]{2,1,0:T(8,128)}, u32[]{:S(2)}) copy-start(f32[1,256,256]{2,1,0:T(8,128)} %param.11) | copy-start | bytes 786436
  187.2 34.3 %copy-start.2 = (f32[1,256,256]{2,1,0:T(8,128)S(1)}, f32[1,256,256]{2,1,0:T(8,128)}, u32[]{:S(2)}) copy-start(f32[1,256,256]{2,1,0:T(8,128)} %param.10) | copy-start | bytes 786436
Sparse Core Ops, SparseCore 0:
  10.8 141.7 all-gather.2
where the time goes:
time: 230 us; the launch traced here: 229 us
  waiting for transfers between devices  112 us (49%)
  blocking collectives  62.4 us (27%)
  local copies, waits for them, and re-layouts  20.8 us (9%)
  between operations  14.1 us (6%)
  matrix products  9.54 us (4%)
  other arithmetic  6.19 us (3%)
  starting transfers between devices  4.38 us (2%)
    all_gather x1, waiting for transfers between devices, shards(): lax.all_gather(grad_rows, TP, axis=0, tiled=True)  111 us
    psum x5, blocking collectives, over_axes(): return functools.reduce(lax.psum, axes, array)  62.4 us
    dot_general x1, local copies, waits for them, and re-layouts, row_adder(): lax.dot_general(inputs, arrived, (((0,), (0,)), ((), ())), preferred_elem...  20.7 us
    dot_general x1, matrix products, row_adder(): lax.dot_general(inputs, arrived, (((0,), (0,)), ((), ())), preferred_elem...  9.54 us
  transfers between devices with their start and end apart: 2, of which 1 were waited for; matrix products, arithmetic and copies ran while one was open for 2% of the time, Pallas kernels for 0%

commit v1 on v0

--- a/solution.py
+++ b/solution.py
@@ -50,7 +50,12 @@
     gain_grad = over_axes(local_terms, DP_TP) / replicas
     inputs = proj_in[0]
     grad_rows = kv_grad[0]
-    local_grad = row_adder(inputs, lax.all_gather(grad_rows, TP, axis=0, tiled=True))
+    local_grad = row_adder(
+        inputs,
+        jnp.concatenate(
+            lax.all_to_all(jnp.stack([grad_rows] * lax.axis_size(TP)), TP, 0, 0), axis=0
+        ),
+    )
     mean_grad = sent_and_summed(local_grad, DP, 1) / replicas
     new_first, new_second, update = adam_update(mean_grad, first_moment[0], second_moment[0])
     firsts = [new_first]

time: 230 us -> 488 us (2.12)
  waiting for transfers between devices: 112 us -> 316 us
  local copies, waits for them, and re-layouts: 20.8 us -> 51 us
  blocking collectives: 62.4 us -> 86.5 us
  between operations: 14.1 us -> 0.73 us
  starting transfers between devices: 4.38 us -> 17.1 us
    all_to_all x0 -> x1, waiting for transfers between devices: none -> 316 us  [shards(): lax.all_to_all(jnp.stack([grad_rows] * lax.axis_size(TP)), TP, 0, 0)]
    all_gather x1 -> x0, waiting for transfers between devices: 111 us -> none  [shards(): lax.all_gather(grad_rows, TP, axis=0, tiled=True)]
    psum x5, blocking collectives: 62.4 us -> 86.5 us  [over_axes(): return functools.reduce(lax.psum, axes, array)]
    all_to_all x0 -> x1, local copies, waits for them, and re-layouts: none -> 22.6 us  [shards(): lax.all_to_all(jnp.stack([grad_rows] * lax.axis_size(TP)), TP, 0, 0)]
    all_to_all x0 -> x1, starting transfers between devices: none -> 12.8 us  [shards(): lax.all_to_all(jnp.stack([grad_rows] * lax.axis_size(TP)), TP, 0, 0)]
    another operation x0 -> x2, local copies, waits for them, and re-layouts: none -> 7.66 us  [the longest x1 6.21 us: shards(): jnp.stack([grad_rows] * lax.axis_size(TP))]
  transfers between devices with their start and end apart: 2 -> 2, of which waited for: 1 -> 1; matrix products, arithmetic and copies ran while one was open for 2% -> 1% of each run, Pallas kernels for 0% -> 0%
where the time goes in v1:
time: 488 us; the launch traced here: 487 us
  waiting for transfers between devices  316 us (65%)
  blocking collectives  86.5 us (18%)
  local copies, waits for them, and re-layouts  51 us (10%)
  starting transfers between devices  17.1 us (4%)
  matrix products  9.54 us (2%)
  other arithmetic  6.19 us (1%)
    all_to_all x1, waiting for transfers between devices, shards(): lax.all_to_all(jnp.stack([grad_rows] * lax.axis_size(TP)), TP, 0, 0)  316 us
    psum x5, blocking collectives, over_axes(): return functools.reduce(lax.psum, axes, array)  86.5 us
    all_to_all x1, local copies, waits for them, and re-layouts, shards(): lax.all_to_all(jnp.stack([grad_rows] * lax.axis_size(TP)), TP, 0, 0)  22.6 us
    dot_general x1, local copies, waits for them, and re-layouts, row_adder(): lax.dot_general(inputs, arrived, (((0,), (0,)), ((), ())), preferred_elem...  20.7 us
    all_to_all x1, starting transfers between devices, shards(): lax.all_to_all(jnp.stack([grad_rows] * lax.axis_size(TP)), TP, 0, 0)  12.8 us
  transfers between devices with their start and end apart: 2, of which 1 were waited for; matrix products, arithmetic and copies ran while one was open for 1% of the time, Pallas kernels for 0%

profile of v1, /device:TPU:1, one launch (start us, length us, event | category | flops | bytes accessed | tf_op | source)
XLA Modules:
  0.0 486.7 jit_solution(9427068252237209626)
XLA Ops:
  0.6 0.0 copy-start
  0.6 1.5 copy.14
  2.1 6.2 %stack.2 = bf16[32,128,2048]{1,2,0:T(8,128)(2,1)} broadcast(bf16[128,2048]{0,1:T(8,128)(2,1)S(1)} %copy.14), dimensions={1,2} | broadcast | bytes 17301504 | tf_op jit(solution)/shard_map/stack | solution.py:56
  8.3 12.8 %all-to-all-start = ((bf16[32,128,2048]{1,2,0:T(8,128)(2,1)}), bf16[32,128,2048]{1,2,0:T(8,128)(2,1)}, u32[]{:S(2)}, u32[]{:S(2)}) async-start(bf16[32,128,2048]{1,2,0:T(8,128)(2,1)} %stack.2), calls=%async_computation | async-start | bytes 33554432 | tf_op jit(solution)/shard_map/all_to_all | solution.py:56
  21.1 2.8 multiply_reduce_fusion
  24.0 14.9 %psum.35 = f32[1,8192]{1,0:T(1,128)S(1)} all-reduce(f32[1,8192]{1,0:T(1,128)S(1)} %bitcast.25), channel_id=1, replica_groups=mesh['dp_0'=4,'dp_1'=2,'tp_0'=2,'tp_1'=8,'tp_2'=2] {'dp_0'}, use_global_device_ids=true, to_apply=%region_2.0 | all-reduce | flops 8192 | bytes 65536 | tf_op jit(solution)/shard_map/psum | solution.py:19
  38.9 14.5 %psum.36 = f32[1,8192]{1,0:T(1,128)S(1)} all-reduce(f32[1,8192]{1,0:T(1,128)S(1)} %psum.35), channel_id=1, replica_groups=mesh['dp_0'=4,'dp_1'=2,'tp_0'=2,'tp_1'=8,'tp_2'=2] {'dp_1'}, use_global_device_ids=true, to_apply=%region_3.0 | all-reduce | flops 8192 | bytes 65536 | tf_op jit(solution)/shard_map/psum | solution.py:19
  53.4 14.9 %psum.37 = f32[1,8192]{1,0:T(1,128)S(1)} all-reduce(f32[1,8192]{1,0:T(1,128)S(1)} %psum.36), channel_id=1, replica_groups=mesh['dp_0'=4,'dp_1'=2,'tp_0'=2,'tp_1'=8,'tp_2'=2] {'tp_0'}, use_global_device_ids=true, to_apply=%region_4.0 | all-reduce | flops 8192 | bytes 65536 | tf_op jit(solution)/shard_map/psum | solution.py:19
  68.3 315.6 %all-to-all-done = bf16[32,128,2048]{1,2,0:T(8,128)(2,1)} async-done(((bf16[32,128,2048]{1,2,0:T(8,128)(2,1)}), bf16[32,128,2048]{1,2,0:T(8,128)(2,1)}, u32[]{:S(2)}, u32[]{:S(2)}) %all-to-all-start) | async-done | bytes 16777248 | tf_op jit(solution)/shard_map/all_to_all | solution.py:56
  383.8 22.6 %copy.15 = bf16[32,128,2048]{2,1,0:T(8,128)(2,1)} copy(bf16[32,128,2048]{1,2,0:T(8,128)(2,1)} %all-to-all-done) | data formatting | bytes 33554432 | tf_op jit(solution)/shard_map/all_to_all | solution.py:56
  406.4 20.7 %copy.16 = bf16[2048,4096]{1,0:T(8,128)(2,1)} copy(bf16[2048,4096]{0,1:T(8,128)(2,1)} %bitcast.22) | data formatting | bytes 33554432 | tf_op jit(solution)/shard_map/dot_general | solution.py:42
  427.2 0.0 copy-done
  427.2 9.5 %fusion.2 = f32[8,256,256]{2,1,0:T(8,128)} fusion(bf16[8,256,4096]{2,1,0:T(8,128)(2,1)} %bitcast.23, bf16[1,4096,256]{2,1,0:T(8,128)(2,1)S(1)} %copy-done), kind=kOutput, calls=%fused_computation.3 | convolution fusion | flops 4294967296 | bytes 20971520 | tf_op jit(solution)/shard_map/dot_general | solution.py:42
  436.7 4.3 all-to-all-start.1
  441.1 0.0 copy-start.1
  441.1 0.0 copy-start.2
  441.1 33.3 %psum.38 = f32[1,8192]{1,0:T(1,128)S(1)} all-reduce(f32[1,8192]{1,0:T(1,128)S(1)} %psum.37), channel_id=1, replica_groups=mesh['dp_0'=4,'dp_1'=2,'tp_0'=2,'tp_1'=8,'tp_2'=2] {'tp_1'}, use_global_device_ids=true, to_apply=%region_5.0 | all-reduce | flops 8192 | bytes 65536 | tf_op jit(solution)/shard_map/psum | solution.py:19
  474.4 8.8 %psum.39 = f32[1,8192]{1,0:T(1,128)S(1)} all-reduce(f32[1,8192]{1,0:T(1,128)S(1)} %psum.38), channel_id=1, replica_groups=mesh['dp_0'=4,'dp_1'=2,'tp_0'=2,'tp_1'=8,'tp_2'=2] {'tp_2'}, use_global_device_ids=true, to_apply=%region_6.0 | all-reduce | flops 8192 | bytes 65536 | tf_op jit(solution)/shard_map/psum | solution.py:19
  483.3 0.6 broadcast_multiply_fusion
  483.9 0.0 all-to-all-done.1
  483.9 1.8 reduce_sum.20
  485.7 0.0 copy-done.1
  485.7 0.0 copy-done.2
  485.7 1.0 add_divide_fusion
Async XLA Ops:
  0.6 426.5 %copy-start = (bf16[1,4096,256]{2,1,0:T(8,128)(2,1)S(1)}, bf16[1,4096,256]{2,1,0:T(8,128)(2,1)}, u32[]{:S(2)}) copy-start(bf16[1,4096,256]{2,1,0:T(8,128)(2,1)} %param.6) | copy-start | bytes 6291460
  8.3 375.5 %all-to-all-start = ((bf16[32,128,2048]{1,2,0:T(8,128)(2,1)}), bf16[32,128,2048]{1,2,0:T(8,128)(2,1)}, u32[]{:S(2)}, u32[]{:S(2)}) async-start(bf16[32,128,2048]{1,2,0:T(8,128)(2,1)} %stack.2), calls=%async_computation | async-start | bytes 33554432 | tf_op jit(solution)/shard_map/all_to_all | solution.py:56
  436.7 47.2 %all-to-all-start.1 = ((f32[8,256,256]{2,1,0:T(8,128)}), f32[8,256,256]{2,1,0:T(8,128)}, u32[]{:S(2)}, u32[]{:S(2)}) async-start(f32[8,256,256]{2,1,0:T(8,128)} %fusion.2), calls=%async_computation.1 | async-start | bytes 4194304 | tf_op jit(solution)/shard_map/all_to_all | solution.py:30
  441.1 44.6 %copy-start.1 = (f32[1,256,256]{2,1,0:T(8,128)S(1)}, f32[1,256,256]{2,1,0:T(8,128)}, u32[]{:S(2)}) copy-start(f32[1,256,256]{2,1,0:T(8,128)} %param.11) | copy-start | bytes 786436
  441.1 44.6 %copy-start.2 = (f32[1,256,256]{2,1,0:T(8,128)S(1)}, f32[1,256,256]{2,1,0:T(8,128)}, u32[]{:S(2)}) copy-start(f32[1,256,256]{2,1,0:T(8,128)} %param.10) | copy-start | bytes 786436
